TPU v7x, 32 devices: a whole 2x2x4 slice. The times are simulated.
32 devices in a mesh: row: 8 (over y, x, core), col: 4 (over z).
Axes of the slice: x: 2, y: 2, z: 4, core: 2. Of those that a mesh axis runs over, the one named last changes fastest.
Arguments:
- blocks: bfloat16 [8, 4, 368, 128, 128], P('row', 'col'), may hold values from -0.125 to 0.125
- block_rows: int32 [8, 4, 368], P('row', 'col'), may hold values from 0 to 31, as said below
- block_cols: int32 [8, 4, 368], P('row', 'col'), may hold values from 0 to 63
- counts: int32 [8, 4], P('row', 'col'), may hold values from 1 to 368, as said below
- features: bfloat16 [32768, 256], P(('col', 'row')), may hold values from -6 to 6
Outputs:
- aggregated: bfloat16 [32768, 256], P(('row', 'col'))
Inputs may be any that keep to these rules, and one draw needn't show every extreme that they name: `block_rows`: within one tile the live slots name distinct pairs of block row and block column. `counts`: some tile holds exactly 368 live blocks in every draw.
All inputs are finite; a program needn't handle non-finite values.
Results may differ from a plain program's by a relative error of at most 0.013.
Values may be sent and summed in bfloat16 or wider, within the bound.
A program may use at most 128 MiB of HBM per device.

v0:
```python
import functools

import jax
import jax.numpy as jnp
from jax import lax
from jax.experimental import pallas as pl
from jax.experimental.pallas import tpu as pltpu
from jax.sharding import PartitionSpec as P

MESH = pl.DeviceIdType.MESH
LANES = 128
HALVES = 2


def bits_for(extent):
    return max(1, (extent - 1).bit_length())


def slot_plan(tile_rows, tile_cols, live_count, row_blocks, slot_bits, col_bits):
    slots = tile_rows.shape[0]
    position = jnp.arange(slots, dtype=jnp.int32)
    row = jnp.where(position < live_count, tile_rows, row_blocks)
    key = (row << slot_bits) + position
    rank = jnp.sum((key[None, :] < key[:, None]).astype(jnp.int32), axis=1)
    packed = (key << col_bits) + tile_cols
    ordered = jnp.sum(jnp.where(rank[:, None] == position[None, :], packed[:, None], 0), axis=0)
    wanted = jnp.arange(row_blocks, dtype=jnp.int32)
    upto = jnp.sum((row[:, None] <= wanted[None, :]).astype(jnp.int32), axis=0)
    here = jnp.sum((row[:, None] == wanted[None, :]).astype(jnp.int32), axis=0)
    last = jnp.where(here > 0, upto - 1, -1)
    return ordered, last


def kernel(
    n_row, n_col, row_blocks, slot_bits, col_bits,
    ordered, last, blocks_hbm, features_hbm, out,
    held, panel0, panel1, sums, part0, part1, right0, right1, left0, left1,
    load_sem, ag_send, ag_recv, rs_send, rs_recv,
):
    panels, parts = (panel0, panel1), (part0, part1)
    rights, lefts = (right0, right1), (left0, left1)
    slots = held.shape[0]
    owned = panel0.shape[0] // n_row
    chunk = row_blocks // n_col
    me = lax.axis_index("row")
    p = lax.axis_index("col")

    fetch = pltpu.make_async_copy(blocks_hbm, held, load_sem.at[HALVES])
    mine = [
        pltpu.make_async_copy(
            features_hbm.at[:, :, pl.ds(h * LANES, LANES)],
            panels[h].at[pl.ds(me * owned, owned)],
            load_sem.at[h],
        )
        for h in range(HALVES)
    ]
    for copy in mine:
        copy.start()
    fetch.start()

    cube = n_row == 8
    core = lax.rem(me, 2)
    if cube:
        x_bit = lax.rem(me // 2, 2)
        y_bit = me // 4
        other = me + 1 - 2 * core
        beside = me + 2 - 4 * x_bit
        above = me + 4 - 8 * y_bit
        across = beside + 4 - 8 * y_bit
        flip = 1 - 2 * core
        mates = [other, beside, above]
    else:
        mates = [lax.rem(me + k, n_row) for k in range(1, n_row)]

    barrier = pltpu.get_barrier_semaphore()
    for mate in mates:
        pl.semaphore_signal(barrier, inc=1, device_id=(mate, p), device_id_type=MESH)

    @pl.when(p > 0)
    def _():
        pl.semaphore_signal(barrier, inc=1, device_id=(me, p - 1), device_id_type=MESH)

    @pl.when(p < n_col - 1)
    def _():
        pl.semaphore_signal(barrier, inc=1, device_id=(me, p + 1), device_id_type=MESH)

    inner = jnp.logical_and(p > 0, p < n_col - 1)

    @pl.when(inner)
    def _():
        pl.semaphore_wait(barrier, len(mates) + 2)

    @pl.when(jnp.logical_not(inner))
    def _():
        pl.semaphore_wait(barrier, len(mates) + 1)

    def shard_copy(h, shard, target, send, recv):
        where = panels[h].at[pl.ds(shard * owned, owned)]
        return pltpu.make_async_remote_copy(
            src_ref=where,
            dst_ref=where,
            send_sem=ag_send.at[h, send],
            recv_sem=ag_recv.at[h, recv],
            device_id=(target, p),
            device_id_type=MESH,
        )

    if cube:
        def first_sends(h):
            shard_copy(h, me, beside, 0, 0).start()
            shard_copy(h, me, above, 1, 1).start()
            shard_copy(h, me, other, 2, 3).start()

        def forward(h):
            @pl.when(core == 0)
            def _():
                shard_copy(h, above, me, 1, 1).wait_recv()
                shard_copy(h, above, beside, 3, 2).start()
                shard_copy(h, above, other, 5, 5).start()
                shard_copy(h, beside, me, 0, 0).wait_recv()
                shard_copy(h, beside, other, 4, 4).start()

            @pl.when(core == 1)
            def _():
                shard_copy(h, beside, me, 0, 0).wait_recv()
                shard_copy(h, beside, above, 3, 2).start()
                shard_copy(h, beside, other, 4, 4).start()
                shard_copy(h, above, me, 1, 1).wait_recv()
                shard_copy(h, above, other, 5, 5).start()

        def gathered(h):
            shard_copy(h, across, me, 2, 2).wait_recv()
            shard_copy(h, across, other, 6, 6).start()
            shard_copy(h, other, me, 2, 3).wait_recv()
            shard_copy(h, beside + flip, me, 4, 4).wait_recv()
            shard_copy(h, above + flip, me, 5, 5).wait_recv()
            shard_copy(h, across + flip, me, 6, 6).wait_recv()

        sends = 7
    else:
        def first_sends(h):
            for k in range(1, n_row):
                shard_copy(h, me, lax.rem(me + k, n_row), k - 1, k - 1).start()

        def forward(h):
            pass

        def gathered(h):
            for k in range(1, n_row):
                shard_copy(h, lax.rem(me + n_row - k, n_row), me, k - 1, k - 1).wait_recv()

        sends = n_row - 1

    def compute(h):
        unroll = 8 if slots % 8 == 0 else 1

        def step(group, carry):
            total, before = carry
            for u in range(unroll):
                place = group * unroll + u
                word = ordered[place]
                row = word >> (slot_bits + col_bits)
                slot = (word >> col_bits) & ((1 << slot_bits) - 1)
                col = word & ((1 << col_bits) - 1)
                product = jnp.dot(held[slot], panels[h][col], preferred_element_type=jnp.float32)
                total = jnp.where(row == before, total, 0.0) + product
                sums[place] = total.astype(jnp.bfloat16)
                before = row
            return total, before

        zero = jnp.zeros((held.shape[1], LANES), jnp.float32)
        lax.fori_loop(0, slots // unroll, step, (zero, jnp.int32(-1)))

        def pick(i, _):
            place = last[i]
            value = sums[jnp.maximum(place, 0)]
            parts[h][i] = jnp.where(place >= 0, value, jnp.zeros_like(value))
            return 0

        lax.fori_loop(0, row_blocks, pick, 0)

    def rs_copy(h, side, d, source):
        land = (rights, lefts)[side][h]
        return pltpu.make_async_remote_copy(
            src_ref=source,
            dst_ref=land.at[d],
            send_sem=rs_send.at[h, side, d],
            recv_sem=rs_recv.at[h, side, d],
            device_id=(me, p + 1 - 2 * side),
            device_id_type=MESH,
        )

    def own(h, d):
        return parts[h].at[pl.ds(d * chunk, chunk)]

    def start_ends(h):
        @pl.when(p == 0)
        def _():
            for d in range(n_col - 1, 0, -1):
                rs_copy(h, 0, d, own(h, d)).start()

        @pl.when(p == n_col - 1)
        def _():
            for d in range(n_col - 1):
                rs_copy(h, 1, d, own(h, d)).start()

    def pass_on(h, side, d):
        land = (rights, lefts)[side][h]
        rs_copy(h, side, d, land.at[d]).wait_recv()

        def add(k, _):
            land[d, k] = (
                land[d, k].astype(jnp.float32) + parts[h][d * chunk + k].astype(jnp.float32)
            ).astype(jnp.bfloat16)
            return 0

        lax.fori_loop(0, chunk, add, 0)
        rs_copy(h, side, d, land.at[d]).start()

    def relay(h):
        for k in range(n_col - 1):
            d = n_col - 1 - k

            relays_left = jnp.logical_and(p > k, p < n_col - 1)
            near_end = p >= n_col // 2

            @pl.when(jnp.logical_and(relays_left, near_end))
            def _():
                pass_on(h, 1, k)

            @pl.when(jnp.logical_and(p > 0, p < d))
            def _():
                pass_on(h, 0, d)

            @pl.when(jnp.logical_and(relays_left, jnp.logical_not(near_end)))
            def _():
                pass_on(h, 1, k)

    def finish(h):
        cols = pl.ds(h * LANES, LANES)

        def total(from_left, from_right):
            if from_left:
                rs_copy(h, 0, p, rights[h].at[p]).wait_recv()
            if from_right:
                rs_copy(h, 1, p, lefts[h].at[p]).wait_recv()

            def add(k, _):
                value = parts[h][p * chunk + k].astype(jnp.float32)
                if from_left:
                    value = value + rights[h][p, k].astype(jnp.float32)
                if from_right:
                    value = value + lefts[h][p, k].astype(jnp.float32)
                out[k, :, cols] = value.astype(jnp.bfloat16)
                return 0

            lax.fori_loop(0, chunk, add, 0)

        pl.when(p == 0)(lambda: total(False, True))
        pl.when(p == n_col - 1)(lambda: total(True, False))
        pl.when(jnp.logical_and(p > 0, p < n_col - 1))(lambda: total(True, True))

    mine[0].wait()
    first_sends(0)
    forward(0)
    mine[1].wait()
    first_sends(1)
    gathered(0)
    fetch.wait()
    compute(0)
    start_ends(0)
    forward(1)
    gathered(1)
    compute(1)
    start_ends(1)
    for h in range(HALVES):
        relay(h)
    for h in range(HALVES):
        finish(h)

    for h in range(HALVES):
        for k in range(sends):
            shard_copy(h, me, me, k, 0).wait_send()
        for d in range(n_col):
            @pl.when(p < d)
            def _():
                rs_copy(h, 0, d, own(h, d)).wait_send()

            @pl.when(p > d)
            def _():
                rs_copy(h, 1, d, own(h, d)).wait_send()


def on_device(n_row, n_col, blocks, block_rows, block_cols, counts, features):
    nodes, width = features.shape
    slots, size = blocks.shape[2], blocks.shape[-1]
    owned = nodes // size
    row_blocks = n_col * owned
    panel_blocks = n_row * owned
    slot_bits, col_bits = bits_for(slots), bits_for(panel_blocks)
    ordered, last = slot_plan(
        block_rows[0, 0], block_cols[0, 0], counts[0, 0], row_blocks, slot_bits, col_bits
    )
    half = (size, LANES)
    vmem = lambda *lead: pltpu.VMEM((*lead, *half), jnp.bfloat16)
    smem = pl.BlockSpec(memory_space=pltpu.SMEM)
    hbm = pl.BlockSpec(memory_space=pl.ANY)
    result = pl.pallas_call(
        functools.partial(kernel, n_row, n_col, row_blocks, slot_bits, col_bits),
        out_shape=jax.ShapeDtypeStruct((owned, size, width), jnp.bfloat16),
        in_specs=[smem, smem, hbm, hbm],
        out_specs=pl.BlockSpec(memory_space=pltpu.VMEM),
        scratch_shapes=[
            pltpu.VMEM((slots, size, size), jnp.bfloat16),
            vmem(panel_blocks), vmem(panel_blocks),
            vmem(slots),
            vmem(row_blocks), vmem(row_blocks),
            vmem(n_col, owned), vmem(n_col, owned), vmem(n_col, owned), vmem(n_col, owned),
            pltpu.SemaphoreType.DMA((HALVES + 1,)),
            pltpu.SemaphoreType.DMA((HALVES, max(7, n_row - 1))),
            pltpu.SemaphoreType.DMA((HALVES, max(7, n_row - 1))),
            pltpu.SemaphoreType.DMA((HALVES, 2, n_col)),
            pltpu.SemaphoreType.DMA((HALVES, 2, n_col)),
        ],
        compiler_params=pltpu.CompilerParams(
            collective_id=0, has_side_effects=True, vmem_limit_bytes=67043328
        ),
    )(ordered, last, blocks.reshape(slots, size, size), features.reshape(owned, size, width))
    return result.reshape(nodes, width)


def solution(mesh):
    return jax.shard_map(
        functools.partial(on_device, mesh.shape["row"], mesh.shape["col"]),
        mesh=mesh,
        in_specs=(
            P("row", "col", None, None, None),
            P("row", "col", None),
            P("row", "col", None),
            P("row", "col"),
            P(("col", "row"), None),
        ),
        out_specs=P(("row", "col"), None),
        check_vma=False,
    )
```

profile of v0, /device:TPU:0, one launch (start us, length us, event | category | flops | bytes accessed | tf_op | source)
XLA Modules:
  0.0 80.3 jit_solution(497467699529996267)
XLA Ops:
  0.7 0.7 reduce
  1.4 0.2 convert_reduce_fusion
  1.6 0.1 convert_reduce_fusion.1
  1.7 0.6 compare_select_fusion.last
  2.3 0.7 reduce.1
  3.0 0.8 select_reduce_fusion.ordered
  3.8 74.7 %shard_map.55 = bf16[8,128,256]{2,1,0:T(8,128)(2,1)} custom-call(s32[368]{0:T(512)} %select_reduce_fusion.ordered, s32[32]{0:T(128)} %compare_select_fusion.last, bf16[368,128,128]{2,1,0:T(8,128)(2,1)} %bitcast.5, bf16[8,128,256]{2,1,0:T(8,128)(2,1)} %bitcast.7), custom_call_target="tpu_custom_call" | custom-call | tf_op jit(solution)/shard_map/pallas_call | solution.py:308
  78.5 1.9 %copy.8 = bf16[1024,256]{1,0:T(8,128)(2,1)} copy(bf16[1024,256]{1,0:T(8,128)(2,1)} %bitcast.6) | data formatting | bytes 1048576
  (2 shorter events, 0.0 us)
where the time goes:
time: 80.6 us; the launch traced here: 80.3 us
  Pallas kernels  74.7 us (93%)
  other arithmetic  3.12 us (4%)
  local copies, waits for them, and re-layouts  1.87 us (2%)
    pallas_call x1, Pallas kernels, on_device(): pl.pallas_call(functools.partial(kernel, n_row, n_col, row_blocks, slot_b...  74.7 us
    unnamed x1, local copies, waits for them, and re-layouts  1.87 us

commit v1 on v0

v1 whole, which is shorter than its diff:
```python
import functools

import jax
import jax.numpy as jnp
from jax import lax
from jax.experimental import pallas as pl
from jax.experimental.pallas import tpu as pltpu
from jax.sharding import PartitionSpec as P

MESH = pl.DeviceIdType.MESH
LANES = 128
HALF = LANES // 2
QUARTERS = 4
GROUP = 40


def bits_for(extent):
    return max(1, (extent - 1).bit_length())


def round_up(value, unit):
    return -(-value // unit) * unit


def kernel(
    n_row, n_col, row_blocks, slot_bits, col_bits, groups,
    rows_in, cols_in, count, blocks_hbm, features_hbm, out,
    held, feat, gath, panel, sums, parts, rights, lefts, plan_vmem, plan,
    load_sem, ag_send, ag_recv, rs_send, rs_recv,
):
    lands = (rights, lefts)
    slots = held.shape[0] - 1
    owned = feat.shape[0]
    half = owned // 2
    width = plan_vmem.shape[1] - round_up(row_blocks, LANES)
    me = lax.axis_index("row")
    p = lax.axis_index("col")

    take = pltpu.make_async_copy(
        features_hbm.at[:, :, pl.ds(0, LANES)], feat, load_sem.at[0]
    )
    mine = [
        pltpu.make_async_copy(
            features_hbm.at[pl.ds(s * half, half), :, pl.ds(LANES, LANES)],
            gath.at[2 + s, pl.ds(me * half, half)],
            load_sem.at[1 + s],
        )
        for s in range(2)
    ]
    fetch = pltpu.make_async_copy(blocks_hbm, held.at[pl.ds(0, slots)], load_sem.at[3])
    take.start()
    for copy in mine:
        copy.start()
    fetch.start()

    cube = n_row == 8
    core = lax.rem(me, 2)
    if cube:
        x_bit = lax.rem(me // 2, 2)
        y_bit = me // 4
        other = me + 1 - 2 * core
        beside = me + 2 - 4 * x_bit
        above = me + 4 - 8 * y_bit
        across = beside + 4 - 8 * y_bit
        flip = 1 - 2 * core
        mates = [other, beside, above]
    else:
        mates = [lax.rem(me + k, n_row) for k in range(1, n_row)]

    barrier = pltpu.get_barrier_semaphore()
    for mate in mates:
        pl.semaphore_signal(barrier, inc=1, device_id=(mate, p), device_id_type=MESH)

    @pl.when(p > 0)
    def _():
        pl.semaphore_signal(barrier, inc=1, device_id=(me, p - 1), device_id_type=MESH)

    @pl.when(p < n_col - 1)
    def _():
        pl.semaphore_signal(barrier, inc=1, device_id=(me, p + 1), device_id_type=MESH)

    low = lax.broadcasted_iota(jnp.int32, (held.shape[1], LANES), 1) < HALF

    def swap(value):
        return pltpu.roll(value, HALF, axis=1)

    held[slots] = jnp.zeros(held.shape[1:], held.dtype)
    take.wait()

    def pack(k, _):
        even = feat[2 * k].astype(jnp.float32)
        odd = feat[2 * k + 1].astype(jnp.float32)
        gath[0, me * half + k] = jnp.where(low, even, swap(odd)).astype(jnp.bfloat16)
        gath[1, me * half + k] = jnp.where(low, swap(even), odd).astype(jnp.bfloat16)
        return 0

    lax.fori_loop(0, half, pack, 0)

    inner = jnp.logical_and(p > 0, p < n_col - 1)

    @pl.when(inner)
    def _():
        pl.semaphore_wait(barrier, len(mates) + 2)

    @pl.when(jnp.logical_not(inner))
    def _():
        pl.semaphore_wait(barrier, len(mates) + 1)

    def shard_copy(m, shard, target, send, recv):
        where = gath.at[m, pl.ds(shard * half, half)]
        return pltpu.make_async_remote_copy(
            src_ref=where,
            dst_ref=where,
            send_sem=ag_send.at[m, send],
            recv_sem=ag_recv.at[m, recv],
            device_id=(target, p),
            device_id_type=MESH,
        )

    def expand(m, shard):
        if m > 1:
            return

        def spread(k, _):
            both = gath[m, shard * half + k].astype(jnp.float32)
            turned = swap(both)
            panel[shard * owned + 2 * k] = jnp.where(low, both, turned).astype(jnp.bfloat16)
            panel[shard * owned + 2 * k + 1] = jnp.where(low, turned, both).astype(jnp.bfloat16)
            return 0

        lax.fori_loop(0, half, spread, 0)

    if cube:
        def first_sends(m):
            shard_copy(m, me, beside, 0, 0).start()
            shard_copy(m, me, above, 1, 1).start()
            shard_copy(m, me, other, 2, 3).start()

        def forward(m):
            @pl.when(core == 0)
            def _():
                shard_copy(m, above, me, 1, 1).wait_recv()
                shard_copy(m, above, beside, 3, 2).start()
                shard_copy(m, above, other, 5, 5).start()
                shard_copy(m, beside, me, 0, 0).wait_recv()
                shard_copy(m, beside, other, 4, 4).start()

            @pl.when(core == 1)
            def _():
                shard_copy(m, beside, me, 0, 0).wait_recv()
                shard_copy(m, beside, above, 3, 2).start()
                shard_copy(m, beside, other, 4, 4).start()
                shard_copy(m, above, me, 1, 1).wait_recv()
                shard_copy(m, above, other, 5, 5).start()

        def gathered(m):
            expand(m, me)
            expand(m, beside)
            expand(m, above)
            shard_copy(m, other, me, 2, 3).wait_recv()
            expand(m, other)
            shard_copy(m, beside + flip, me, 4, 4).wait_recv()
            expand(m, beside + flip)
            shard_copy(m, above + flip, me, 5, 5).wait_recv()
            expand(m, above + flip)
            shard_copy(m, across, me, 2, 2).wait_recv()
            shard_copy(m, across, other, 6, 6).start()
            expand(m, across)
            shard_copy(m, across + flip, me, 6, 6).wait_recv()
            expand(m, across + flip)

        sends = 7
    else:
        def first_sends(m):
            for k in range(1, n_row):
                shard_copy(m, me, lax.rem(me + k, n_row), k - 1, k - 1).start()

        def forward(m):
            pass

        def gathered(m):
            expand(m, me)
            for k in range(1, n_row):
                shard = lax.rem(me + n_row - k, n_row)
                shard_copy(m, shard, me, k - 1, k - 1).wait_recv()
                expand(m, shard)

        sends = n_row - 1

    def make_plan():
        def iota(shape, axis):
            return lax.broadcasted_iota(jnp.int32, shape, axis)

        def over_lanes(value):
            return jnp.sum(value.astype(jnp.float32), axis=1, keepdims=True).astype(jnp.int32)

        def over_rows(value):
            return jnp.sum(value, axis=0, keepdims=True)

        square = (slots, slots)
        wide = plan_vmem.shape[1] - width
        row = jnp.where(iota((1, slots), 1) < count[0, 0], rows_in[...], row_blocks)
        eye = iota(square, 0) == iota(square, 1)
        row_down = over_lanes(jnp.where(eye, row, 0))
        col_down = over_lanes(jnp.where(eye, cols_in[...], 0))
        ahead = jnp.logical_and(row == row_down, iota(square, 1) < iota(square, 0))
        rank = over_lanes(jnp.where(ahead, 1, 0))
        line = iota((slots, wide), 1)
        here = over_rows(jnp.where(line == row_down, 1, 0))
        pairs = jnp.where(iota((1, wide), 1) < row_blocks, (here + 1) >> 1, 0)
        before = over_lanes(jnp.where(line < row_down, pairs, 0))
        place = jnp.where(row_down < row_blocks, 2 * before + rank, -1)
        spare = (row_blocks << (slot_bits + col_bits)) + (slots << col_bits)
        packed = (row_down << (slot_bits + col_bits)) + (iota((slots, 1), 0) << col_bits) + col_down
        hit = place == iota((slots, width), 1)
        plan_vmem[:, pl.ds(0, width)] = spare + over_rows(jnp.where(hit, packed - spare, 0))
        small = (wide, wide)
        pairs_down = over_lanes(jnp.where(iota(small, 0) == iota(small, 1), pairs, 0))
        upto = over_rows(jnp.where(iota(small, 0) <= iota(small, 1), pairs_down, 0))
        plan_vmem[:, pl.ds(width, wide)] = jnp.where(here > 0, upto - 1, -1)

    to_scalar = pltpu.make_async_copy(plan_vmem, plan, load_sem.at[4])

    def compute(piece, hooks):
        def tile(word):
            col = word & ((1 << col_bits) - 1)
            if piece < 2:
                return panel[col]
            block = lax.rem(col, owned)
            shard = col // owned
            return gath[2 + block // half, shard * half + lax.rem(block, half)]

        def step(pair, carry):
            total, before = carry
            first = plan[0, 2 * pair]
            second = plan[0, 2 * pair + 1]
            row = first >> (slot_bits + col_bits)
            slot = lambda word: (word >> col_bits) & ((1 << slot_bits) - 1)
            left = jnp.concatenate([held[slot(first)], held[slot(second)]], axis=1)
            right = jnp.concatenate([tile(first), tile(second)], axis=0)
            product = jnp.dot(left, right, preferred_element_type=jnp.float32)
            total = jnp.where(row == before, total, 0.0) + product
            sums[pair] = total.astype(jnp.bfloat16)
            return total, row

        def group(g, carry):
            return lax.fori_loop(
                0, GROUP, lambda u, c: step(g * GROUP + u, c), carry, unroll=True
            )

        carry = (jnp.zeros((held.shape[1], LANES), jnp.float32), jnp.int32(-1))
        start = 0
        for stop, hook in hooks + [(groups, None)]:
            carry = lax.fori_loop(start, stop, group, carry)
            if hook is not None:
                hook()
            start = stop

    def row_sum(i):
        at = plan[0, width + i]
        value = sums[jnp.maximum(at, 0)]
        return jnp.where(at >= 0, value, jnp.zeros_like(value))

    def rs_copy(m, side, d, source):
        return pltpu.make_async_remote_copy(
            src_ref=source,
            dst_ref=lands[side].at[m, d],
            send_sem=rs_send.at[m, side, d],
            recv_sem=rs_recv.at[m, side, d],
            device_id=(me, p + 1 - 2 * side),
            device_id_type=MESH,
        )

    def emit(members):
        for k in range(n_col):
            d = jnp.where(p == n_col - 1, k, n_col - 1 - k)
            for m in members:
                def pick(u, _):
                    if m < 2:
                        value = jnp.where(
                            low, row_sum(d * owned + 2 * u), row_sum(d * owned + 2 * u + 1)
                        )
                    else:
                        value = row_sum(d * owned + (m - 2) * half + u)
                    parts[m, d, u] = value
                    return 0

                lax.fori_loop(0, half, pick, 0)

                @pl.when(jnp.logical_and(p == 0, d > 0))
                def _():
                    rs_copy(m, 0, d, parts.at[m, d]).start()

                @pl.when(jnp.logical_and(p == n_col - 1, d < n_col - 1))
                def _():
                    rs_copy(m, 1, d, parts.at[m, d]).start()

    def pass_on(m, side, d):
        land = lands[side]
        rs_copy(m, side, d, land.at[m, d]).wait_recv()

        def add(k, _):
            land[m, d, k] = (
                land[m, d, k].astype(jnp.float32) + parts[m, d, k].astype(jnp.float32)
            ).astype(jnp.bfloat16)
            return 0

        lax.fori_loop(0, half, add, 0)
        rs_copy(m, side, d, land.at[m, d]).start()

    def relay(members):
        near_end = p >= n_col // 2

        def rightward(k, here):
            d = n_col - 1 - k
            if 0 <= k and d > 1:
                @pl.when(jnp.logical_and(jnp.logical_and(p > 0, p < d), here))
                def _():
                    for m in members:
                        pass_on(m, 0, d)

        def leftward(k, here):
            if 0 <= k < n_col - 2:
                @pl.when(jnp.logical_and(jnp.logical_and(p > k, p < n_col - 1), here))
                def _():
                    for m in members:
                        pass_on(m, 1, k)

        for k in range(n_col):
            rightward(k, jnp.logical_not(near_end))
            leftward(k, near_end)
            leftward(k - 1, jnp.logical_not(near_end))
            rightward(k - 1, near_end)

    def finish(members):
        def total(from_left, from_right):
            for m in members:
                if from_left:
                    rs_copy(m, 0, p, rights.at[m, p]).wait_recv()
                if from_right:
                    rs_copy(m, 1, p, lefts.at[m, p]).wait_recv()

            def whole(m, k):
                value = parts[m, p, k].astype(jnp.float32)
                if from_left:
                    value = value + rights[m, p, k].astype(jnp.float32)
                if from_right:
                    value = value + lefts[m, p, k].astype(jnp.float32)
                return value

            def add(k, _):
                if members == (0, 1):
                    first, second = whole(0, k), whole(1, k)
                    at = pl.ds(0, LANES)
                    out[2 * k, :, at] = jnp.where(low, first, swap(second)).astype(jnp.bfloat16)
                    out[2 * k + 1, :, at] = jnp.where(low, swap(first), second).astype(jnp.bfloat16)
                else:
                    for m in members:
                        at = pl.ds(LANES, LANES)
                        out[(m - 2) * half + k, :, at] = whole(m, k).astype(jnp.bfloat16)
                return 0

            lax.fori_loop(0, half, add, 0)

        pl.when(p == 0)(lambda: total(False, True))
        pl.when(p == n_col - 1)(lambda: total(True, False))
        pl.when(jnp.logical_and(p > 0, p < n_col - 1))(lambda: total(True, True))

    def later_1():
        forward(1)
        first_sends(3)

    first_sends(0)
    make_plan()
    to_scalar.start()
    forward(0)
    first_sends(1)
    for copy in mine:
        copy.wait()
    first_sends(2)
    to_scalar.wait()
    gathered(0)
    fetch.wait()
    cut = max(0, groups - 2)
    compute(0, [(cut, later_1)])
    emit((0,))
    forward(2)
    gathered(1)
    compute(1, [(cut, lambda: forward(3))])
    emit((1,))
    relay((0,))
    gathered(2)
    gathered(3)
    compute(2, [])
    emit((2, 3))
    relay((1,))
    finish((0, 1))
    relay((2, 3))
    finish((2,))
    finish((3,))

    for m in range(QUARTERS):
        for k in range(sends):
            shard_copy(m, me, me, k, 0).wait_send()
        for d in range(n_col):
            @pl.when(p < d)
            def _():
                rs_copy(m, 0, d, parts.at[m, d]).wait_send()

            @pl.when(p > d)
            def _():
                rs_copy(m, 1, d, parts.at[m, d]).wait_send()


def on_device(n_row, n_col, blocks, block_rows, block_cols, counts, features):
    nodes, width = features.shape
    slots, size = blocks.shape[2], blocks.shape[-1]
    owned = nodes // size
    half = owned // 2
    row_blocks = n_col * owned
    panel_blocks = n_row * owned
    slot_bits, col_bits = bits_for(slots + 1), bits_for(panel_blocks)
    most = (slots + min(slots, row_blocks)) // 2
    groups = -(-most // GROUP)
    pairs = groups * GROUP
    planned = round_up(2 * pairs, LANES) + round_up(row_blocks, LANES)
    vmem = lambda *lead: pltpu.VMEM((*lead, size, LANES), jnp.bfloat16)
    smem = pl.BlockSpec(memory_space=pltpu.SMEM)
    near = pl.BlockSpec(memory_space=pltpu.VMEM)
    hbm = pl.BlockSpec(memory_space=pl.ANY)
    links = max(7, n_row - 1)
    result = pl.pallas_call(
        functools.partial(kernel, n_row, n_col, row_blocks, slot_bits, col_bits, groups),
        out_shape=jax.ShapeDtypeStruct((owned, size, width), jnp.bfloat16),
        in_specs=[near, near, smem, hbm, hbm],
        out_specs=near,
        scratch_shapes=[
            vmem(slots + 1),
            vmem(owned),
            vmem(QUARTERS, n_row * half),
            vmem(panel_blocks),
            vmem(pairs),
            vmem(QUARTERS, n_col, half),
            vmem(QUARTERS, n_col, half),
            vmem(QUARTERS, n_col, half),
            pltpu.VMEM((1, planned), jnp.int32),
            pltpu.SMEM((1, planned), jnp.int32),
            pltpu.SemaphoreType.DMA((5,)),
            pltpu.SemaphoreType.DMA((QUARTERS, links)),
            pltpu.SemaphoreType.DMA((QUARTERS, links)),
            pltpu.SemaphoreType.DMA((QUARTERS, 2, n_col)),
            pltpu.SemaphoreType.DMA((QUARTERS, 2, n_col)),
        ],
        compiler_params=pltpu.CompilerParams(
            collective_id=0, has_side_effects=True, vmem_limit_bytes=67043328
        ),
    )(
        block_rows.reshape(1, slots),
        block_cols.reshape(1, slots),
        counts,
        blocks.reshape(slots, size, size),
        features.reshape(owned, size, width),
    )
    return result.reshape(nodes, width)


def solution(mesh):
    return jax.shard_map(
        functools.partial(on_device, mesh.shape["row"], mesh.shape["col"]),
        mesh=mesh,
        in_specs=(
            P("row", "col", None, None, None),
            P("row", "col", None),
            P("row", "col", None),
            P("row", "col"),
            P(("col", "row"), None),
        ),
        out_specs=P(("row", "col"), None),
        check_vma=False,
    )
```

time: 80.6 us -> 68.2 us (0.85)
  Pallas kernels: 74.7 us -> 65.5 us
  other arithmetic: 3.12 us -> 0 us
    pallas_call x1, Pallas kernels: 74.7 us -> 65.5 us  [on_device(): pl.pallas_call(functools.partial(kernel, n_row, n_col, row_blocks, slot_b...]
    unnamed x2 -> x0, other arithmetic: 1.4 us -> none
    reduce_sum x3 -> x0, other arithmetic: 1.11 us -> none  [the longest x1 0.76 us: slot_plan(): jnp.sum(jnp.where(rank[:, None] == position[None, :], packed[:, None], 0)...]
where the time goes in v1:
time: 68.2 us; the launch traced here: 68 us
  Pallas kernels  65.5 us (96%)
  local copies, waits for them, and re-layouts  1.87 us (3%)
    pallas_call x1, Pallas kernels, on_device(): pl.pallas_call(functools.partial(kernel, n_row, n_col, row_blocks, slot_b...  65.5 us
    unnamed x1, local copies, waits for them, and re-layouts  1.87 us

profile of v1, /device:TPU:0, one launch (start us, length us, event | category | flops | bytes accessed | tf_op | source)
XLA Modules:
  0.0 68.0 jit_solution(10948499716803309474)
XLA Ops:
  0.7 65.5 %shard_map.55 = bf16[8,128,256]{2,1,0:T(8,128)(2,1)} custom-call(s32[1,368]{1,0:T(1,128)} %bitcast.8, s32[1,368]{1,0:T(1,128)} %bitcast.9, s32[1,1]{1,0:T(1,128)S(6)} %copy.7.count, bf16[368,128,128]{2,1,0:T(8,128)(2,1)} %bitcast.5, bf16[8,128,256]{2,1,0:T(8,128)(2,1)} %bitcast.7), custom_call_target="tpu_custom_call" | custom-call | tf_op jit(solution)/shard_map/pallas_call | solution.py:432
  66.2 1.9 %copy.8 = bf16[1024,256]{1,0:T(8,128)(2,1)} copy(bf16[1024,256]{1,0:T(8,128)(2,1)} %bitcast.6) | data formatting | bytes 1048576

commit v2 on v1

--- a/solution.py
+++ b/solution.py
@@ -25,13 +25,14 @@
 def kernel(
     n_row, n_col, row_blocks, slot_bits, col_bits, groups,
     rows_in, cols_in, count, blocks_hbm, features_hbm, out,
-    held, feat, gath, panel, sums, parts, rights, lefts, plan_vmem, plan,
+    held, feat, gath, wide, panel, result, sums, parts, rights, lefts, plan_vmem, plan,
     load_sem, ag_send, ag_recv, rs_send, rs_recv,
 ):
     lands = (rights, lefts)
     slots = held.shape[0] - 1
     owned = feat.shape[0]
     half = owned // 2
+    part = half // 2
     width = plan_vmem.shape[1] - round_up(row_blocks, LANES)
     me = lax.axis_index("row")
     p = lax.axis_index("col")
@@ -42,7 +43,7 @@
     mine = [
         pltpu.make_async_copy(
             features_hbm.at[pl.ds(s * half, half), :, pl.ds(LANES, LANES)],
-            gath.at[2 + s, pl.ds(me * half, half)],
+            wide.at[pl.ds(me * owned + s * half, half)],
             load_sem.at[1 + s],
         )
         for s in range(2)
@@ -106,8 +107,13 @@
     def _():
         pl.semaphore_wait(barrier, len(mates) + 1)
 
-    def shard_copy(m, shard, target, send, recv):
-        where = gath.at[m, pl.ds(shard * half, half)]
+    def shard_of(m, shard, first, count):
+        if m < 2:
+            return gath.at[m, pl.ds(shard * half + first, count)]
+        return wide.at[pl.ds(shard * owned + (m - 2) * half + first, count)]
+
+    def shard_copy(m, shard, target, send, recv, first=0, count=half):
+        where = shard_of(m, shard, first, count)
         return pltpu.make_async_remote_copy(
             src_ref=where,
             dst_ref=where,
@@ -134,24 +140,22 @@
         def first_sends(m):
             shard_copy(m, me, beside, 0, 0).start()
             shard_copy(m, me, above, 1, 1).start()
+
+        def own_chip(m):
             shard_copy(m, me, other, 2, 3).start()
 
         def forward(m):
-            @pl.when(core == 0)
-            def _():
-                shard_copy(m, above, me, 1, 1).wait_recv()
-                shard_copy(m, above, beside, 3, 2).start()
-                shard_copy(m, above, other, 5, 5).start()
-                shard_copy(m, beside, me, 0, 0).wait_recv()
-                shard_copy(m, beside, other, 4, 4).start()
-
-            @pl.when(core == 1)
-            def _():
-                shard_copy(m, beside, me, 0, 0).wait_recv()
-                shard_copy(m, beside, above, 3, 2).start()
-                shard_copy(m, beside, other, 4, 4).start()
-                shard_copy(m, above, me, 1, 1).wait_recv()
-                shard_copy(m, above, other, 5, 5).start()
+            shard_copy(m, above, me, 1, 1).wait_recv()
+            shard_copy(m, above, beside, 3, 2, 0, part).start()
+            shard_copy(m, above, other, 5, 5).start()
+            shard_copy(m, beside, me, 0, 0).wait_recv()
+            shard_copy(m, beside, above, 7, 7, part, half - part).start()
+            shard_copy(m, beside, other, 4, 4).start()
+
+        def cross(m):
+            shard_copy(m, across, me, 2, 2, 0, part).wait_recv()
+            shard_copy(m, across, me, 7, 7, part, half - part).wait_recv()
+            shard_copy(m, across, other, 6, 6).start()
 
         def gathered(m):
             expand(m, me)
@@ -163,19 +167,30 @@
             expand(m, beside + flip)
             shard_copy(m, above + flip, me, 5, 5).wait_recv()
             expand(m, above + flip)
-            shard_copy(m, across, me, 2, 2).wait_recv()
-            shard_copy(m, across, other, 6, 6).start()
+            if m < 2:
+                cross(m)
             expand(m, across)
             shard_copy(m, across + flip, me, 6, 6).wait_recv()
             expand(m, across + flip)
 
-        sends = 7
+        def sent(m):
+            for k in (0, 1, 2, 4, 5, 6):
+                shard_copy(m, me, me, k, 0).wait_send()
+            shard_copy(m, me, me, 3, 0, 0, part).wait_send()
+            shard_copy(m, me, me, 7, 0, part, half - part).wait_send()
+
     else:
         def first_sends(m):
             for k in range(1, n_row):
                 shard_copy(m, me, lax.rem(me + k, n_row), k - 1, k - 1).start()
 
+        def own_chip(m):
+            pass
+
         def forward(m):
+            pass
+
+        def cross(m):
             pass
 
         def gathered(m):
@@ -185,7 +200,9 @@
                 shard_copy(m, shard, me, k - 1, k - 1).wait_recv()
                 expand(m, shard)
 
-        sends = n_row - 1
+        def sent(m):
+            for k in range(n_row - 1):
+                shard_copy(m, me, me, k, 0).wait_send()
 
     def make_plan():
         def iota(shape, axis):
@@ -198,37 +215,33 @@
             return jnp.sum(value, axis=0, keepdims=True)
 
         square = (slots, slots)
-        wide = plan_vmem.shape[1] - width
+        rest = plan_vmem.shape[1] - width
         row = jnp.where(iota((1, slots), 1) < count[0, 0], rows_in[...], row_blocks)
         eye = iota(square, 0) == iota(square, 1)
         row_down = over_lanes(jnp.where(eye, row, 0))
         col_down = over_lanes(jnp.where(eye, cols_in[...], 0))
         ahead = jnp.logical_and(row == row_down, iota(square, 1) < iota(square, 0))
         rank = over_lanes(jnp.where(ahead, 1, 0))
-        line = iota((slots, wide), 1)
+        line = iota((slots, rest), 1)
         here = over_rows(jnp.where(line == row_down, 1, 0))
-        pairs = jnp.where(iota((1, wide), 1) < row_blocks, (here + 1) >> 1, 0)
+        pairs = jnp.where(iota((1, rest), 1) < row_blocks, (here + 1) >> 1, 0)
         before = over_lanes(jnp.where(line < row_down, pairs, 0))
         place = jnp.where(row_down < row_blocks, 2 * before + rank, -1)
         spare = (row_blocks << (slot_bits + col_bits)) + (slots << col_bits)
         packed = (row_down << (slot_bits + col_bits)) + (iota((slots, 1), 0) << col_bits) + col_down
         hit = place == iota((slots, width), 1)
         plan_vmem[:, pl.ds(0, width)] = spare + over_rows(jnp.where(hit, packed - spare, 0))
-        small = (wide, wide)
+        small = (rest, rest)
         pairs_down = over_lanes(jnp.where(iota(small, 0) == iota(small, 1), pairs, 0))
         upto = over_rows(jnp.where(iota(small, 0) <= iota(small, 1), pairs_down, 0))
-        plan_vmem[:, pl.ds(width, wide)] = jnp.where(here > 0, upto - 1, -1)
+        plan_vmem[:, pl.ds(width, rest)] = jnp.where(here > 0, upto - 1, -1)
 
     to_scalar = pltpu.make_async_copy(plan_vmem, plan, load_sem.at[4])
 
     def compute(piece, hooks):
         def tile(word):
             col = word & ((1 << col_bits) - 1)
-            if piece < 2:
-                return panel[col]
-            block = lax.rem(col, owned)
-            shard = col // owned
-            return gath[2 + block // half, shard * half + lax.rem(block, half)]
+            return panel[col] if piece < 2 else wide[col]
 
         def step(pair, carry):
             total, before = carry
@@ -308,29 +321,43 @@
         lax.fori_loop(0, half, add, 0)
         rs_copy(m, side, d, land.at[m, d]).start()
 
-    def relay(members):
-        near_end = p >= n_col // 2
-
-        def rightward(k, here):
-            d = n_col - 1 - k
-            if 0 <= k and d > 1:
-                @pl.when(jnp.logical_and(jnp.logical_and(p > 0, p < d), here))
-                def _():
-                    for m in members:
-                        pass_on(m, 0, d)
-
-        def leftward(k, here):
-            if 0 <= k < n_col - 2:
-                @pl.when(jnp.logical_and(jnp.logical_and(p > k, p < n_col - 1), here))
-                def _():
-                    for m in members:
-                        pass_on(m, 1, k)
-
-        for k in range(n_col):
-            rightward(k, jnp.logical_not(near_end))
-            leftward(k, near_end)
-            leftward(k - 1, jnp.logical_not(near_end))
-            rightward(k - 1, near_end)
+    near_end = p >= n_col // 2
+
+    def rightward(m, k, here):
+        d = n_col - 1 - k
+        if d > 1:
+            @pl.when(jnp.logical_and(jnp.logical_and(p > 0, p < d), here))
+            def _():
+                pass_on(m, 0, d)
+
+    def leftward(m, k, here):
+        if k < n_col - 2:
+            @pl.when(jnp.logical_and(jnp.logical_and(p > k, p < n_col - 1), here))
+            def _():
+                pass_on(m, 1, k)
+
+    def primary(m, k):
+        rightward(m, k, jnp.logical_not(near_end))
+        leftward(m, k, near_end)
+
+    def secondary(m, k):
+        leftward(m, k, jnp.logical_not(near_end))
+        rightward(m, k, near_end)
+
+    def rest(m):
+        secondary(m, 0)
+        for k in range(2, n_col):
+            primary(m, k)
+            secondary(m, k - 1)
+
+    def leave(members):
+        if members == (0, 1):
+            rows, at = pl.ds(0, owned), pl.ds(0, LANES)
+        else:
+            rows, at = pl.ds((members[0] - 2) * half, half), pl.ds(LANES, LANES)
+        return pltpu.make_async_copy(
+            result.at[rows, :, at], out.at[rows, :, at], load_sem.at[5 + members[0]]
+        )
 
     def finish(members):
         def total(from_left, from_right):
@@ -352,12 +379,12 @@
                 if members == (0, 1):
                     first, second = whole(0, k), whole(1, k)
                     at = pl.ds(0, LANES)
-                    out[2 * k, :, at] = jnp.where(low, first, swap(second)).astype(jnp.bfloat16)
-                    out[2 * k + 1, :, at] = jnp.where(low, swap(first), second).astype(jnp.bfloat16)
+                    result[2 * k, :, at] = jnp.where(low, first, swap(second)).astype(jnp.bfloat16)
+                    result[2 * k + 1, :, at] = jnp.where(low, swap(first), second).astype(jnp.bfloat16)
                 else:
                     for m in members:
                         at = pl.ds(LANES, LANES)
-                        out[(m - 2) * half + k, :, at] = whole(m, k).astype(jnp.bfloat16)
+                        result[(m - 2) * half + k, :, at] = whole(m, k).astype(jnp.bfloat16)
                 return 0
 
             lax.fori_loop(0, half, add, 0)
@@ -365,12 +392,20 @@
         pl.when(p == 0)(lambda: total(False, True))
         pl.when(p == n_col - 1)(lambda: total(True, False))
         pl.when(jnp.logical_and(p > 0, p < n_col - 1))(lambda: total(True, True))
-
-    def later_1():
+        leave(members).start()
+
+    def late_0():
         forward(1)
         first_sends(3)
-
+        own_chip(3)
+
+    def late_1():
+        forward(3)
+        primary(0, 0)
+
+    cut = max(0, groups - 2)
     first_sends(0)
+    own_chip(0)
     make_plan()
     to_scalar.start()
     forward(0)
@@ -380,28 +415,38 @@
     first_sends(2)
     to_scalar.wait()
     gathered(0)
+    own_chip(1)
+    own_chip(2)
     fetch.wait()
-    cut = max(0, groups - 2)
-    compute(0, [(cut, later_1)])
+    compute(0, [(cut, late_0)])
     emit((0,))
     forward(2)
     gathered(1)
-    compute(1, [(cut, lambda: forward(3))])
+    compute(1, [(cut, late_1), (groups - 1, lambda: cross(2))])
     emit((1,))
-    relay((0,))
+    primary(0, 1)
     gathered(2)
+    cross(3)
     gathered(3)
-    compute(2, [])
+    rest(0)
+    compute(2, [(groups - 1, lambda: primary(1, 0))])
     emit((2, 3))
-    relay((1,))
+    primary(1, 1)
+    rest(1)
     finish((0, 1))
-    relay((2, 3))
+    primary(2, 0)
+    primary(3, 0)
+    primary(2, 1)
+    rest(2)
+    primary(3, 1)
+    rest(3)
     finish((2,))
     finish((3,))
+    for members in ((0, 1), (2,), (3,)):
+        leave(members).wait()
 
     for m in range(QUARTERS):
-        for k in range(sends):
-            shard_copy(m, me, me, k, 0).wait_send()
+        sent(m)
         for d in range(n_col):
             @pl.when(p < d)
             def _():
@@ -428,24 +473,26 @@
     smem = pl.BlockSpec(memory_space=pltpu.SMEM)
     near = pl.BlockSpec(memory_space=pltpu.VMEM)
     hbm = pl.BlockSpec(memory_space=pl.ANY)
-    links = max(7, n_row - 1)
+    links = max(8, n_row - 1)
     result = pl.pallas_call(
         functools.partial(kernel, n_row, n_col, row_blocks, slot_bits, col_bits, groups),
         out_shape=jax.ShapeDtypeStruct((owned, size, width), jnp.bfloat16),
         in_specs=[near, near, smem, hbm, hbm],
-        out_specs=near,
+        out_specs=hbm,
         scratch_shapes=[
             vmem(slots + 1),
             vmem(owned),
-            vmem(QUARTERS, n_row * half),
+            vmem(2, n_row * half),
             vmem(panel_blocks),
+            vmem(panel_blocks),
+            pltpu.VMEM((owned, size, width), jnp.bfloat16),
             vmem(pairs),
             vmem(QUARTERS, n_col, half),
             vmem(QUARTERS, n_col, half),
             vmem(QUARTERS, n_col, half),
             pltpu.VMEM((1, planned), jnp.int32),
             pltpu.SMEM((1, planned), jnp.int32),
-            pltpu.SemaphoreType.DMA((5,)),
+            pltpu.SemaphoreType.DMA((9,)),
             pltpu.SemaphoreType.DMA((QUARTERS, links)),
             pltpu.SemaphoreType.DMA((QUARTERS, links)),
             pltpu.SemaphoreType.DMA((QUARTERS, 2, n_col)),

time: 68.2 us -> 58.7 us (0.86)
  Pallas kernels: 65.5 us -> 56 us
    pallas_call x1, Pallas kernels: 65.5 us -> 56 us  [on_device(): pl.pallas_call(functools.partial(kernel, n_row, n_col, row_blocks, slot_b...]
where the time goes in v2:
time: 58.7 us; the launch traced here: 58.5 us
  Pallas kernels  56 us (95%)
  local copies, waits for them, and re-layouts  1.87 us (3%)
  between operations  0.66 us (1%)
    pallas_call x1, Pallas kernels, on_device(): pl.pallas_call(functools.partial(kernel, n_row, n_col, row_blocks, slot_b...  56 us
    unnamed x1, local copies, waits for them, and re-layouts  1.87 us

profile of v2, /device:TPU:0, one launch (start us, length us, event | category | flops | bytes accessed | tf_op | source)
XLA Modules:
  0.0 58.5 jit_solution(16038911007094510974)
XLA Ops:
  0.7 56.0 %shard_map.55 = bf16[8,128,256]{2,1,0:T(8,128)(2,1)} custom-call(s32[1,368]{1,0:T(1,128)} %bitcast.8, s32[1,368]{1,0:T(1,128)} %bitcast.9, s32[1,1]{1,0:T(1,128)S(6)} %copy.7.count, bf16[368,128,128]{2,1,0:T(8,128)(2,1)} %bitcast.5, bf16[8,128,256]{2,1,0:T(8,128)(2,1)} %bitcast.7), custom_call_target="tpu_custom_call" | custom-call | tf_op jit(solution)/shard_map/pallas_call | solution.py:477
  56.6 1.9 %copy.8 = bf16[1024,256]{1,0:T(8,128)(2,1)} copy(bf16[1024,256]{1,0:T(8,128)(2,1)} %bitcast.6) | data formatting | bytes 1048576

commit v3 on v2

--- a/solution.py
+++ b/solution.py
@@ -24,8 +24,8 @@
 
 def kernel(
     n_row, n_col, row_blocks, slot_bits, col_bits, groups,
-    rows_in, cols_in, count, blocks_hbm, features_hbm, out,
-    held, feat, gath, wide, panel, result, sums, parts, rights, lefts, plan_vmem, plan,
+    rows_hbm, cols_hbm, count, blocks_hbm, features_hbm, out,
+    held, feat, gath, wide, panel, sums, parts, rights, lefts, slots_in, plan_vmem, plan,
     load_sem, ag_send, ag_recv, rs_send, rs_recv,
 ):
     lands = (rights, lefts)
@@ -49,8 +49,12 @@
         for s in range(2)
     ]
     fetch = pltpu.make_async_copy(blocks_hbm, held.at[pl.ds(0, slots)], load_sem.at[3])
+    listed = [
+        pltpu.make_async_copy(rows_hbm, slots_in.at[0], load_sem.at[5]),
+        pltpu.make_async_copy(cols_hbm, slots_in.at[1], load_sem.at[6]),
+    ]
     take.start()
-    for copy in mine:
+    for copy in listed + mine:
         copy.start()
     fetch.start()
 
@@ -85,18 +89,19 @@
     def swap(value):
         return pltpu.roll(value, HALF, axis=1)
 
-    held[slots] = jnp.zeros(held.shape[1:], held.dtype)
     take.wait()
 
-    def pack(k, _):
-        even = feat[2 * k].astype(jnp.float32)
-        odd = feat[2 * k + 1].astype(jnp.float32)
-        gath[0, me * half + k] = jnp.where(low, even, swap(odd)).astype(jnp.bfloat16)
-        gath[1, me * half + k] = jnp.where(low, swap(even), odd).astype(jnp.bfloat16)
-        return 0
-
-    lax.fori_loop(0, half, pack, 0)
-
+    def pack(m):
+        def one(k, _):
+            even = feat[2 * k].astype(jnp.float32)
+            odd = feat[2 * k + 1].astype(jnp.float32)
+            even, odd = (even, swap(odd)) if m == 0 else (swap(even), odd)
+            gath[m, me * half + k] = jnp.where(low, even, odd).astype(jnp.bfloat16)
+            return 0
+
+        lax.fori_loop(0, half, one, 0)
+
+    pack(0)
     inner = jnp.logical_and(p > 0, p < n_col - 1)
 
     @pl.when(inner)
@@ -137,28 +142,38 @@
         lax.fori_loop(0, half, spread, 0)
 
     if cube:
+        ahead, behind = (0, part), (part, half - part)
+
         def first_sends(m):
-            shard_copy(m, me, beside, 0, 0).start()
-            shard_copy(m, me, above, 1, 1).start()
+            shard_copy(m, me, above, 1, 1, *ahead).start()
+            shard_copy(m, me, beside, 0, 0, *behind).start()
+            shard_copy(m, me, above, 9, 9, *behind).start()
+            shard_copy(m, me, beside, 8, 8, *ahead).start()
 
         def own_chip(m):
             shard_copy(m, me, other, 2, 3).start()
 
         def forward(m):
-            shard_copy(m, above, me, 1, 1).wait_recv()
-            shard_copy(m, above, beside, 3, 2, 0, part).start()
+            shard_copy(m, above, me, 1, 1, *ahead).wait_recv()
+            shard_copy(m, above, beside, 3, 2, *ahead).start()
+            shard_copy(m, beside, me, 0, 0, *behind).wait_recv()
+            shard_copy(m, beside, above, 7, 7, *behind).start()
+
+        def arrived(m):
+            shard_copy(m, above, me, 9, 9, *behind).wait_recv()
             shard_copy(m, above, other, 5, 5).start()
-            shard_copy(m, beside, me, 0, 0).wait_recv()
-            shard_copy(m, beside, above, 7, 7, part, half - part).start()
+            shard_copy(m, beside, me, 8, 8, *ahead).wait_recv()
             shard_copy(m, beside, other, 4, 4).start()
 
         def cross(m):
-            shard_copy(m, across, me, 2, 2, 0, part).wait_recv()
-            shard_copy(m, across, me, 7, 7, part, half - part).wait_recv()
+            shard_copy(m, across, me, 2, 2, *ahead).wait_recv()
+            shard_copy(m, across, me, 7, 7, *behind).wait_recv()
             shard_copy(m, across, other, 6, 6).start()
 
         def gathered(m):
             expand(m, me)
+            if m < 2:
+                arrived(m)
             expand(m, beside)
             expand(m, above)
             shard_copy(m, other, me, 2, 3).wait_recv()
@@ -174,10 +189,12 @@
             expand(m, across + flip)
 
         def sent(m):
-            for k in (0, 1, 2, 4, 5, 6):
+            for k in (2, 4, 5, 6):
                 shard_copy(m, me, me, k, 0).wait_send()
-            shard_copy(m, me, me, 3, 0, 0, part).wait_send()
-            shard_copy(m, me, me, 7, 0, part, half - part).wait_send()
+            for k in (1, 3, 8):
+                shard_copy(m, me, me, k, 0, *ahead).wait_send()
+            for k in (0, 7, 9):
+                shard_copy(m, me, me, k, 0, *behind).wait_send()
 
     else:
         def first_sends(m):
@@ -191,6 +208,9 @@
             pass
 
         def cross(m):
+            pass
+
+        def arrived(m):
             pass
 
         def gathered(m):
@@ -216,10 +236,10 @@
 
         square = (slots, slots)
         rest = plan_vmem.shape[1] - width
-        row = jnp.where(iota((1, slots), 1) < count[0, 0], rows_in[...], row_blocks)
+        row = jnp.where(iota((1, slots), 1) < count[0, 0], slots_in[0], row_blocks)
         eye = iota(square, 0) == iota(square, 1)
         row_down = over_lanes(jnp.where(eye, row, 0))
-        col_down = over_lanes(jnp.where(eye, cols_in[...], 0))
+        col_down = over_lanes(jnp.where(eye, slots_in[1], 0))
         ahead = jnp.logical_and(row == row_down, iota(square, 1) < iota(square, 0))
         rank = over_lanes(jnp.where(ahead, 1, 0))
         line = iota((slots, rest), 1)
@@ -350,15 +370,6 @@
             primary(m, k)
             secondary(m, k - 1)
 
-    def leave(members):
-        if members == (0, 1):
-            rows, at = pl.ds(0, owned), pl.ds(0, LANES)
-        else:
-            rows, at = pl.ds((members[0] - 2) * half, half), pl.ds(LANES, LANES)
-        return pltpu.make_async_copy(
-            result.at[rows, :, at], out.at[rows, :, at], load_sem.at[5 + members[0]]
-        )
-
     def finish(members):
         def total(from_left, from_right):
             for m in members:
@@ -379,12 +390,12 @@
                 if members == (0, 1):
                     first, second = whole(0, k), whole(1, k)
                     at = pl.ds(0, LANES)
-                    result[2 * k, :, at] = jnp.where(low, first, swap(second)).astype(jnp.bfloat16)
-                    result[2 * k + 1, :, at] = jnp.where(low, swap(first), second).astype(jnp.bfloat16)
+                    out[2 * k, :, at] = jnp.where(low, first, swap(second)).astype(jnp.bfloat16)
+                    out[2 * k + 1, :, at] = jnp.where(low, swap(first), second).astype(jnp.bfloat16)
                 else:
                     for m in members:
                         at = pl.ds(LANES, LANES)
-                        result[(m - 2) * half + k, :, at] = whole(m, k).astype(jnp.bfloat16)
+                        out[(m - 2) * half + k, :, at] = whole(m, k).astype(jnp.bfloat16)
                 return 0
 
             lax.fori_loop(0, half, add, 0)
@@ -392,7 +403,6 @@
         pl.when(p == 0)(lambda: total(False, True))
         pl.when(p == n_col - 1)(lambda: total(True, False))
         pl.when(jnp.logical_and(p > 0, p < n_col - 1))(lambda: total(True, True))
-        leave(members).start()
 
     def late_0():
         forward(1)
@@ -401,13 +411,18 @@
 
     def late_1():
         forward(3)
+        arrived(3)
         primary(0, 0)
 
     cut = max(0, groups - 2)
     first_sends(0)
     own_chip(0)
+    for copy in listed:
+        copy.wait()
     make_plan()
     to_scalar.start()
+    pack(1)
+    held[slots] = jnp.zeros(held.shape[1:], held.dtype)
     forward(0)
     first_sends(1)
     for copy in mine:
@@ -421,6 +436,7 @@
     compute(0, [(cut, late_0)])
     emit((0,))
     forward(2)
+    arrived(2)
     gathered(1)
     compute(1, [(cut, late_1), (groups - 1, lambda: cross(2))])
     emit((1,))
@@ -442,9 +458,6 @@
     rest(3)
     finish((2,))
     finish((3,))
-    for members in ((0, 1), (2,), (3,)):
-        leave(members).wait()
-
     for m in range(QUARTERS):
         sent(m)
         for d in range(n_col):
@@ -470,26 +483,30 @@
     pairs = groups * GROUP
     planned = round_up(2 * pairs, LANES) + round_up(row_blocks, LANES)
     vmem = lambda *lead: pltpu.VMEM((*lead, size, LANES), jnp.bfloat16)
-    smem = pl.BlockSpec(memory_space=pltpu.SMEM)
     near = pl.BlockSpec(memory_space=pltpu.VMEM)
-    hbm = pl.BlockSpec(memory_space=pl.ANY)
-    links = max(8, n_row - 1)
+    far = lambda value: pltpu.with_memory_space_constraint(value, pltpu.HBM)
+    hbm = pl.BlockSpec(memory_space=pltpu.HBM)
+    scratch = size * LANES * 2 * (
+        slots + 1 + owned + 2 * n_row * half + 2 * panel_blocks + pairs + 3 * QUARTERS * n_col * half
+    )
+    limit = scratch + (2 << 20)
+    links = max(10, n_row - 1)
     result = pl.pallas_call(
         functools.partial(kernel, n_row, n_col, row_blocks, slot_bits, col_bits, groups),
         out_shape=jax.ShapeDtypeStruct((owned, size, width), jnp.bfloat16),
-        in_specs=[near, near, smem, hbm, hbm],
-        out_specs=hbm,
+        in_specs=[hbm, hbm, pl.BlockSpec(memory_space=pltpu.SMEM), hbm, hbm],
+        out_specs=near,
         scratch_shapes=[
             vmem(slots + 1),
             vmem(owned),
             vmem(2, n_row * half),
             vmem(panel_blocks),
             vmem(panel_blocks),
-            pltpu.VMEM((owned, size, width), jnp.bfloat16),
             vmem(pairs),
             vmem(QUARTERS, n_col, half),
             vmem(QUARTERS, n_col, half),
             vmem(QUARTERS, n_col, half),
+            pltpu.VMEM((2, 1, slots), jnp.int32),
             pltpu.VMEM((1, planned), jnp.int32),
             pltpu.SMEM((1, planned), jnp.int32),
             pltpu.SemaphoreType.DMA((9,)),
@@ -499,14 +516,14 @@
             pltpu.SemaphoreType.DMA((QUARTERS, 2, n_col)),
         ],
         compiler_params=pltpu.CompilerParams(
-            collective_id=0, has_side_effects=True, vmem_limit_bytes=67043328
+            collective_id=0, has_side_effects=True, vmem_limit_bytes=limit
         ),
     )(
-        block_rows.reshape(1, slots),
-        block_cols.reshape(1, slots),
+        far(block_rows.reshape(1, slots)),
+        far(block_cols.reshape(1, slots)),
         counts,
-        blocks.reshape(slots, size, size),
-        features.reshape(owned, size, width),
+        far(blocks.reshape(slots, size, size)),
+        far(features.reshape(owned, size, width)),
     )
     return result.reshape(nodes, width)
 

time: 58.7 us -> 55.9 us (0.952)
  Pallas kernels: 56 us -> 54.3 us
  local copies, waits for them, and re-layouts: 1.87 us -> 0.8 us
    pallas_call x1, Pallas kernels: 56 us -> 54.3 us  [on_device(): pl.pallas_call(functools.partial(kernel, n_row, n_col, row_blocks, slot_b...]
    unnamed x1, local copies, waits for them, and re-layouts: 1.87 us -> 0.8 us
where the time goes in v3:
time: 55.9 us; the launch traced here: 55.7 us
  Pallas kernels  54.3 us (97%)
  local copies, waits for them, and re-layouts  0.8 us (1%)
  between operations  0.66 us (1%)
    pallas_call x1, Pallas kernels, on_device(): pl.pallas_call(functools.partial(kernel, n_row, n_col, row_blocks, slot_b...  54.3 us

profile of v3, /device:TPU:0, one launch (start us, length us, event | category | flops | bytes accessed | tf_op | source)
XLA Modules:
  0.0 55.7 jit_solution(13392370711984420002)
XLA Ops:
  0.7 54.3 %shard_map.55 = bf16[8,128,256]{2,1,0:T(8,128)(2,1)S(1)} custom-call(s32[1,368]{1,0:T(1,128)} %bitcast.8, s32[1,368]{1,0:T(1,128)} %bitcast.9, s32[1,1]{1,0:T(1,128)S(6)} %copy.7.count, bf16[368,128,128]{2,1,0:T(8,128)(2,1)} %bitcast.6, bf16[8,128,256]{2,1,0:T(8,128)(2,1)} %bitcast.7), custom_call_target="tpu_custom_call" | custom-call | tf_op jit(solution)/shard_map/pallas_call | solution.py:494
  54.9 0.8 %copy.8 = bf16[1024,256]{1,0:T(8,128)(2,1)} copy(bf16[1024,256]{1,0:T(8,128)(2,1)S(1)} %bitcast.5) | data formatting | bytes 1048576
